TPU v7x, 256 devices: a whole 4x4x8 slice. The times are simulated.
256 devices in a mesh: gx: 4 (over x), gy: 8 (over y, core), gz: 8 (over z).
Axes of the slice: x: 4, y: 4, z: 8, core: 2. Of those that a mesh axis runs over, the one named last changes fastest.
Arguments:
- right_side: float32 [8, 32, 256, 1024], P(None, 'gx', 'gy', 'gz'), may hold values from -12 to 12
- shift: float32 [32, 256, 1024], P('gx', 'gy', 'gz'), may hold values from 0.02 to 2
Outputs:
- solution_block: float32 [8, 32, 256, 1024], P(None, 'gx', 'gy', 'gz')
- residual_norms: float32 [8], replicated
All inputs are finite; a program needn't handle non-finite values.
Results may differ from a plain program's by a relative error of at most 0.0003.
Values sent between devices are 32-bit elements; how exact they have to be, the bound alone decides.
A program may use at most 128 MiB of HBM per device.

v0:
```python
import jax
import jax.numpy as jnp
from jax import lax
from jax.sharding import Mesh
from jax.sharding import PartitionSpec as P

ITERS = 2
GX_GY_GZ = ("gx", "gy_0", "gy_1", "gz")
GY = ("gy_0", "gy_1")


def padded_2(value, sides, width):
    edges = {}
    for axis, dim in sides:
        devices, length = (lax.axis_size(axis), value.shape[dim])
        up = [(i, (i + 1) % devices) for i in range(devices - 1)]
        last = lax.slice_in_dim(value, length - width, length, axis=dim)
        leading = lax.slice_in_dim(value, 0, width, axis=dim)
        edges[dim] = (
            lax.ppermute(last, axis, up),
            lax.ppermute(leading, axis, [(b, a) for a, b in up]),
        )
    done = []
    for _, dim in sides:
        low, high = edges[dim]
        around = [(width, width) if d in done else (0, 0) for d in range(value.ndim)]
        value = jnp.concatenate([jnp.pad(low, around), value, jnp.pad(high, around)], axis=dim)
        done.append(dim)
    return value


def by_axis(value, axes):
    for axis in axes:
        value = lax.psum(value, axis)
    return value


def operate(fields, shift):
    padded = padded_2(fields, (("gx", 1), (GY, 2), ("gz", 3)), 1)
    beside = padded[:, 2:, 1:-1, 1:-1] + padded[:, :-2, 1:-1, 1:-1]
    beside = beside + padded[:, 1:-1, 2:, 1:-1] + padded[:, 1:-1, :-2, 1:-1]
    beside = beside + padded[:, 1:-1, 1:-1, 2:] + padded[:, 1:-1, 1:-1, :-2]
    return (6.0 + shift)[None] * fields - beside


def lower_inverse(lower):
    count = lower.shape[0]
    return jax.scipy.linalg.solve_triangular(lower, jnp.eye(count, dtype=lower.dtype), lower=True)


def small_dot(left, right):
    return jnp.dot(left, right, precision=lax.Precision.HIGHEST)


def body(right_side, shift):
    width = right_side.shape[0]
    shape = right_side.shape
    rows = right_side.reshape(width, -1)
    first_step = None
    images = operate(right_side, shift).reshape(width, -1)
    both = jnp.concatenate([rows, images], axis=0)
    joint = by_axis(small_dot(both, both.T), GX_GY_GZ)
    lower = jnp.linalg.cholesky(joint[:width, :width])
    start_coeff = lower.T
    inverse = lower_inverse(lower)
    first_basis = small_dot(inverse, rows)
    basis = [first_basis]
    first_image = small_dot(inverse, images)
    first_coeffs = small_dot(small_dot(inverse, joint[:width, width:]), inverse.T)
    first_self = small_dot(small_dot(inverse, joint[width:, width:]), inverse.T)
    first_gram = first_self - small_dot(first_coeffs.T, first_coeffs)
    first_projected = first_image - small_dot(first_coeffs.T, first_basis)
    first_step = (first_coeffs, first_gram, first_projected)
    hessen = jnp.zeros(((ITERS + 1) * width, ITERS * width), jnp.float32)
    for step in range(ITERS):
        if step == 0 and first_step is not None:
            coeffs, gram, projected = first_step
        else:
            image = operate(basis[step].reshape(shape), shift).reshape(width, -1)
            stacked = jnp.concatenate(basis, axis=0)
            products = by_axis(
                small_dot(jnp.concatenate([stacked, image], axis=0), image.T), GX_GY_GZ
            )
            coeffs = products[:-width]
            gram = products[-width:] - small_dot(coeffs.T, coeffs)
            projected = image - small_dot(coeffs.T, stacked)
        lower = jnp.linalg.cholesky(gram)
        hessen = hessen.at[: (step + 1) * width, step * width : (step + 1) * width].set(coeffs)
        hessen = hessen.at[
            (step + 1) * width : (step + 2) * width, step * width : (step + 1) * width
        ].set(lower.T)
        if step + 1 < ITERS:
            basis.append(small_dot(lower_inverse(lower), projected))
    target = jnp.zeros(((ITERS + 1) * width, width), jnp.float32).at[:width].set(start_coeff)
    normal = small_dot(hessen.T, hessen)
    factor = jnp.linalg.cholesky(normal)
    coeff_y = jax.scipy.linalg.cho_solve((factor, True), small_dot(hessen.T, target))
    solution = small_dot(coeff_y.T, jnp.concatenate(basis, axis=0)).reshape(shape)
    leftover = target - small_dot(hessen, coeff_y)
    norms = jnp.sqrt(jnp.sum(leftover * leftover, axis=0))
    return (solution, norms)


def solution(mesh):
    split = Mesh(
        mesh.devices.reshape(mesh.shape["gx"], 4, 2, mesh.shape["gz"]), ("gx", "gy_0", "gy_1", "gz")
    )
    return jax.shard_map(
        body,
        mesh=split,
        in_specs=(P(None, "gx", GY, "gz"), P("gx", GY, "gz")),
        out_specs=(P(None, "gx", GY, "gz"), P()),
        check_vma=False,
    )
```

profile of v0, /device:TPU:8, one launch (start us, length us, event | category | flops | bytes accessed | tf_op | source)
XLA Modules:
  0.0 174.2 jit_solution(10873587700840309843)
XLA Ops:
  0.6 1.7 fusion.68
  2.3 3.4 %collective-permute-start.1 = (f32[8,1,32,128]{3,2,1,0:T(8,128)}, f32[8,1,32,128]{3,2,1,0:T(8,128)S(1)}, u32[]{:S(2)}, u32[]{:S(2)}) collective-permute-start(f32[8,1,32,128]{3,2,1,0:T(8,128)} %get-tuple-element.79), channel_id=1, source_target_pairs={{0,64},{64,128},{128,192},{1,65},{65,129},{129,193},{2,66},{66,130... | collective-permute-start | bytes 393224 | tf_op jit(solution)/shard_map/ppermute | solution.py:20
  5.7 1.9 %fusion.66 = (f32[8,8,32,1]{3,2,1,0:T(8,128)S(1)}, f32[8,8,32,1]{3,2,1,0:T(8,128)S(1)}) fusion(f32[8,8,32,128]{3,2,1,0:T(8,128)} %param.15), kind=kLoop, calls=%fused_computation.126 | loop fusion | bytes 32768 | tf_op jit(solution)/shard_map/slice | solution.py:18
  7.7 1.0 copy.56
  8.7 1.3 collective-permute-start.4
  10.0 1.0 copy.57
  11.0 4.7 %collective-permute-start.5 = (f32[8,8,32,1]{2,1,3,0:T(8,128)}, f32[8,8,32,1]{2,1,3,0:T(8,128)S(1)}, u32[]{:S(2)}, u32[]{:S(2)}) collective-permute-start(f32[8,8,32,1]{2,1,3,0:T(8,128)} %copy.57), channel_id=1, source_target_pairs={{0,1},{1,2},{2,3},{3,4},{4,5},{5,6},{6,7},{8,9},{9,10},{10,11},{11... | collective-permute-start | bytes 24584 | tf_op jit(solution)/shard_map/ppermute | solution.py:20
  15.8 1.9 %collective-permute-start.2 = (f32[8,8,1,128]{3,2,1,0:T(1,128)S(1)}, f32[8,8,1,128]{3,2,1,0:T(1,128)S(1)}, u32[]{:S(2)}, u32[]{:S(2)}) collective-permute-start(f32[8,8,1,128]{3,2,1,0:T(1,128)S(1)} %get-tuple-element.77), channel_id=1, source_target_pairs={{8,0},{16,8},{24,16},{32,24},{40,32},{48,40},{56,48},{9,1},{17,9},... | collective-permute-start | bytes 98312 | tf_op jit(solution)/shard_map/ppermute | solution.py:21
  17.7 2.4 %collective-permute-start.3 = (f32[8,8,1,128]{3,2,1,0:T(1,128)S(1)}, f32[8,8,1,128]{3,2,1,0:T(1,128)S(1)}, u32[]{:S(2)}, u32[]{:S(2)}) collective-permute-start(f32[8,8,1,128]{3,2,1,0:T(1,128)S(1)} %get-tuple-element.76), channel_id=1, source_target_pairs={{0,8},{8,16},{16,24},{24,32},{32,40},{40,48},{48,56},{1,9},{9,17},... | collective-permute-start | bytes 98312 | tf_op jit(solution)/shard_map/ppermute | solution.py:20
  20.8 1.3 collective-permute-start
  22.1 2.2 %copy.60 = f32[8,8,32,1]{3,2,1,0:T(8,128)} copy(f32[8,8,32,1]{2,1,3,0:T(8,128)} %collective-permute-done.4) | data formatting | bytes 16384
  24.3 1.4 copy.61
  25.9 2.9 %collective-permute-done = f32[8,1,32,128]{3,2,1,0:T(8,128)S(1)} collective-permute-done((f32[8,1,32,128]{3,2,1,0:T(8,128)S(1)}, f32[8,1,32,128]{3,2,1,0:T(8,128)S(1)}, u32[]{:S(2)}, u32[]{:S(2)}) %collective-permute-start) | collective-permute-done | bytes 131104 | tf_op jit(solution)/shard_map/ppermute | solution.py:21
  28.9 1.2 fusion.26
  30.7 2.9 %fusion.6 = f32[16,16]{0,1:T(8,128)S(1)} fusion(f32[8,32768]{1,0:T(8,128)S(1)} %bitcast.94, f32[8,32768]{1,0:T(8,128)S(1)} %bitcast.92), kind=kOutput, calls=%fused_computation.7 | convolution fusion | flops 101187584 | bytes 2098176 | tf_op jit(solution)/shard_map/dot_general | solution.py:52
  33.5 10.3 %psum.56 = f32[16,16]{0,1:T(8,128)S(1)} all-reduce(f32[16,16]{0,1:T(8,128)S(1)} %fusion.6), channel_id=1, replica_groups=mesh['gx'=4,'gy_0'=4,'gy_1'=2,'gz'=8] {'gx'}, use_global_device_ids=true, to_apply=%region_0.1 | all-reduce | flops 256 | bytes 2048 | tf_op jit(solution)/shard_map/psum | solution.py:34
  43.8 8.8 %psum.57 = f32[16,16]{0,1:T(8,128)S(1)} all-reduce(f32[16,16]{0,1:T(8,128)S(1)} %psum.56), channel_id=1, replica_groups=mesh['gx'=4,'gy_0'=4,'gy_1'=2,'gz'=8] {'gy_0'}, use_global_device_ids=true, to_apply=%region_1.2 | all-reduce | flops 256 | bytes 2048 | tf_op jit(solution)/shard_map/psum | solution.py:34
  52.6 2.5 %psum.58 = f32[16,16]{0,1:T(8,128)S(1)} all-reduce(f32[16,16]{0,1:T(8,128)S(1)} %psum.57), channel_id=1, replica_groups=mesh['gx'=4,'gy_0'=4,'gy_1'=2,'gz'=8] {'gy_1'}, use_global_device_ids=true, to_apply=%region_2.3 | all-reduce | flops 256 | bytes 2048 | tf_op jit(solution)/shard_map/psum | solution.py:34
  55.1 19.4 %psum.59 = f32[16,16]{0,1:T(8,128)S(1)} all-reduce(f32[16,16]{0,1:T(8,128)S(1)} %psum.58), channel_id=1, replica_groups=mesh['gx'=4,'gy_0'=4,'gy_1'=2,'gz'=8] {'gz'}, use_global_device_ids=true, to_apply=%region_3.4 | all-reduce | flops 256 | bytes 2048 | tf_op jit(solution)/shard_map/psum | solution.py:34
  74.6 0.7 cholesky.94
  75.3 0.6 compare_reduce_fusion.2
  76.0 0.6 fusion.55
  76.6 0.6 custom-call.17
  77.6 1.5 fusion.62
  79.1 1.5 fusion.61
  81.3 0.7 cholesky.105
  82.0 0.6 compare_reduce_fusion.1
  82.7 0.6 select_bitcast_fusion.1
  83.3 0.6 custom-call.18
  84.2 1.0 convolution_subtract_fusion
  85.2 1.0 fusion.72
  86.3 1.7 fusion.63
  88.0 0.7 fusion.65
  88.8 1.7 collective-permute-start.7
  90.5 0.7 fusion.64
  91.2 1.7 copy.58
  92.8 1.3 collective-permute-start.10
  94.1 2.3 %copy.59 = f32[8,8,32,1]{2,1,3,0:T(8,128)} copy(f32[8,8,32,1]{3,0,2,1:T(8,128)} %get-tuple-element.69) | data formatting | bytes 16384
  96.4 5.1 %collective-permute-start.11 = (f32[8,8,32,1]{2,1,3,0:T(8,128)}, f32[8,8,32,1]{2,1,3,0:T(8,128)}, u32[]{:S(2)}, u32[]{:S(2)}) collective-permute-start(f32[8,8,32,1]{2,1,3,0:T(8,128)} %copy.59), channel_id=1, source_target_pairs={{0,1},{1,2},{2,3},{3,4},{4,5},{5,6},{6,7},{8,9},{9,10},{10,11},{11... | collective-permute-start | bytes 24584 | tf_op jit(solution)/shard_map/ppermute | solution.py:20
  101.5 1.9 %collective-permute-start.8 = (f32[8,8,1,128]{3,2,1,0:T(1,128)}, f32[8,8,1,128]{3,2,1,0:T(1,128)}, u32[]{:S(2)}, u32[]{:S(2)}) collective-permute-start(f32[8,8,1,128]{3,2,1,0:T(1,128)} %get-tuple-element.71), channel_id=1, source_target_pairs={{8,0},{16,8},{24,16},{32,24},{40,32},{48,40},{56,48},{9,1},{17,9},... | collective-permute-start | bytes 98312 | tf_op jit(solution)/shard_map/ppermute | solution.py:21
  103.5 2.4 %collective-permute-start.9 = (f32[8,8,1,128]{3,2,1,0:T(1,128)}, f32[8,8,1,128]{3,2,1,0:T(1,128)}, u32[]{:S(2)}, u32[]{:S(2)}) collective-permute-start(f32[8,8,1,128]{3,2,1,0:T(1,128)} %get-tuple-element.70), channel_id=1, source_target_pairs={{0,8},{8,16},{16,24},{24,32},{32,40},{40,48},{48,56},{1,9},{9,17},... | collective-permute-start | bytes 98312 | tf_op jit(solution)/shard_map/ppermute | solution.py:20
  106.5 0.7 and_reduce_fusion
  107.6 1.5 collective-permute-start.6
  109.1 2.2 %copy.62 = f32[8,8,32,1]{3,2,1,0:T(8,128)} copy(f32[8,8,32,1]{2,1,3,0:T(8,128)} %collective-permute-done.10) | data formatting | bytes 16384
  111.3 2.2 %copy.63 = f32[8,8,32,1]{3,2,1,0:T(8,128)} copy(f32[8,8,32,1]{2,1,3,0:T(8,128)} %collective-permute-done.11) | data formatting | bytes 16384
  113.5 0.8 pad.51
  114.3 0.8 pad.52
  116.6 1.2 fusion.18
  118.4 3.0 %fusion = f32[24,8]{0,1:T(8,128)S(1)} fusion(f32[8,32768]{1,0:T(8,128)S(1)} %bitcast.96, f32[8,32768]{1,0:T(8,128)S(1)} %fusion.72, f32[8,32768]{1,0:T(8,128)S(1)} %fusion.61), kind=kOutput, calls=%fused_computation.1 | convolution fusion | flops 77070336 | bytes 3146496 | tf_op jit(solution)/shard_map/dot_general | solution.py:52
  121.4 10.4 %psum.60 = f32[24,8]{0,1:T(8,128)S(1)} all-reduce(f32[24,8]{0,1:T(8,128)S(1)} %fusion), channel_id=1, replica_groups=mesh['gx'=4,'gy_0'=4,'gy_1'=2,'gz'=8] {'gx'}, use_global_device_ids=true, to_apply=%region_7.10 | all-reduce | flops 192 | bytes 1536 | tf_op jit(solution)/shard_map/psum | solution.py:34
  131.8 10.7 %psum.61 = f32[24,8]{0,1:T(8,128)S(1)} all-reduce(f32[24,8]{0,1:T(8,128)S(1)} %psum.60), channel_id=1, replica_groups=mesh['gx'=4,'gy_0'=4,'gy_1'=2,'gz'=8] {'gy_0'}, use_global_device_ids=true, to_apply=%region_8.11 | all-reduce | flops 192 | bytes 1536 | tf_op jit(solution)/shard_map/psum | solution.py:34
  142.5 2.5 %psum.62 = f32[24,8]{0,1:T(8,128)S(1)} all-reduce(f32[24,8]{0,1:T(8,128)S(1)} %psum.61), channel_id=1, replica_groups=mesh['gx'=4,'gy_0'=4,'gy_1'=2,'gz'=8] {'gy_1'}, use_global_device_ids=true, to_apply=%region_9.12 | all-reduce | flops 192 | bytes 1536 | tf_op jit(solution)/shard_map/psum | solution.py:34
  144.9 15.0 %psum.63 = f32[24,8]{0,1:T(8,128)S(1)} all-reduce(f32[24,8]{0,1:T(8,128)S(1)} %psum.62), channel_id=1, replica_groups=mesh['gx'=4,'gy_0'=4,'gy_1'=2,'gz'=8] {'gz'}, use_global_device_ids=true, to_apply=%region_10.13 | all-reduce | flops 192 | bytes 1536 | tf_op jit(solution)/shard_map/psum | solution.py:34
  160.1 0.7 cholesky.116
  160.9 0.6 compare_reduce_fusion
  161.5 0.6 select_bitcast_fusion
  162.2 2.0 %dynamic-slice_select_fusion = f32[16,8]{0,1:T(8,128)S(1)} fusion(f32[24,16]{0,1:T(8,128)S(1)} %scatter.19, s32[]{:T(128)} %bitcast.8, s32[]{:T(128)} %bitcast.9, f32[24,8]{0,1:T(8,128)S(1)} %psum.63, pred[]{:T(512)} %and_reduce_fusion), kind=kLoop, calls=%fused_computation.105 | loop fusion | flops 128 | bytes 1545 | tf_op jit(solution)/shard_map/select.25
  164.1 1.7 scatter.20
  166.6 1.5 cholesky.41
  168.1 0.6 compare_reduce_fusion.3
  168.7 0.6 fusion.32
  169.4 1.2 custom-call.15
  171.4 1.1 fusion.10
  173.0 1.2 copy.51
  (71 shorter events, 8.5 us)
Async XLA Ops:
  2.3 23.5 %collective-permute-start.1 = (f32[8,1,32,128]{3,2,1,0:T(8,128)}, f32[8,1,32,128]{3,2,1,0:T(8,128)S(1)}, u32[]{:S(2)}, u32[]{:S(2)}) collective-permute-start(f32[8,1,32,128]{3,2,1,0:T(8,128)} %get-tuple-element.79), channel_id=1, source_target_pairs={{0,64},{64,128},{128,192},{1,65},{65,129},{129,193},{2,66},{66,130... | collective-permute-start | bytes 393224 | tf_op jit(solution)/shard_map/ppermute | solution.py:20
  7.6 8.1 %copy-start = (f32[8,8,32,128]{3,2,1,0:T(8,128)S(1)}, f32[8,8,32,128]{3,2,1,0:T(8,128)}, u32[]{:S(2)}) copy-start(f32[8,8,32,128]{3,2,1,0:T(8,128)} %param.15) | copy-start | bytes 3145732
  7.6 12.5 %copy-start.5 = (f32[8,32,128]{2,1,0:T(8,128)S(1)}, f32[8,32,128]{2,1,0:T(8,128)}, u32[]{:S(2)}) copy-start(f32[8,32,128]{2,1,0:T(8,128)} %param.16) | copy-start | bytes 393220
  8.7 12.1 %collective-permute-start.4 = (f32[8,8,32,1]{2,1,3,0:T(8,128)}, f32[8,8,32,1]{2,1,3,0:T(8,128)}, u32[]{:S(2)}, u32[]{:S(2)}) collective-permute-start(f32[8,8,32,1]{2,1,3,0:T(8,128)} %copy.56), channel_id=1, source_target_pairs={{1,0},{2,1},{3,2},{4,3},{5,4},{6,5},{7,6},{9,8},{10,9},{11,10},{12... | collective-permute-start | bytes 24584 | tf_op jit(solution)/shard_map/ppermute | solution.py:21
  11.0 9.8 %copy-start.6 = (f32[8,1,32,128]{3,2,1,0:T(8,128)S(1)}, f32[8,1,32,128]{3,2,1,0:T(8,128)}, u32[]{:S(2)}) copy-start(f32[8,1,32,128]{3,2,1,0:T(8,128)} %get-tuple-element.78) | copy-start | bytes 393220
  11.0 13.3 %collective-permute-start.5 = (f32[8,8,32,1]{2,1,3,0:T(8,128)}, f32[8,8,32,1]{2,1,3,0:T(8,128)S(1)}, u32[]{:S(2)}, u32[]{:S(2)}) collective-permute-start(f32[8,8,32,1]{2,1,3,0:T(8,128)} %copy.57), channel_id=1, source_target_pairs={{0,1},{1,2},{2,3},{3,4},{4,5},{5,6},{6,7},{8,9},{9,10},{10,11},{11... | collective-permute-start | bytes 24584 | tf_op jit(solution)/shard_map/ppermute | solution.py:20
  15.8 10.0 %collective-permute-start.2 = (f32[8,8,1,128]{3,2,1,0:T(1,128)S(1)}, f32[8,8,1,128]{3,2,1,0:T(1,128)S(1)}, u32[]{:S(2)}, u32[]{:S(2)}) collective-permute-start(f32[8,8,1,128]{3,2,1,0:T(1,128)S(1)} %get-tuple-element.77), channel_id=1, source_target_pairs={{8,0},{16,8},{24,16},{32,24},{40,32},{48,40},{56,48},{9,1},{17,9},... | collective-permute-start | bytes 98312 | tf_op jit(solution)/shard_map/ppermute | solution.py:21
  17.7 8.1 %collective-permute-start.3 = (f32[8,8,1,128]{3,2,1,0:T(1,128)S(1)}, f32[8,8,1,128]{3,2,1,0:T(1,128)S(1)}, u32[]{:S(2)}, u32[]{:S(2)}) collective-permute-start(f32[8,8,1,128]{3,2,1,0:T(1,128)S(1)} %get-tuple-element.76), channel_id=1, source_target_pairs={{0,8},{8,16},{16,24},{24,32},{32,40},{40,48},{48,56},{1,9},{9,17},... | collective-permute-start | bytes 98312 | tf_op jit(solution)/shard_map/ppermute | solution.py:20
  20.8 8.0 %collective-permute-start = (f32[8,1,32,128]{3,2,1,0:T(8,128)S(1)}, f32[8,1,32,128]{3,2,1,0:T(8,128)S(1)}, u32[]{:S(2)}, u32[]{:S(2)}) collective-permute-start(f32[8,1,32,128]{3,2,1,0:T(8,128)S(1)} %copy-done.6), channel_id=1, source_target_pairs={{64,0},{128,64},{192,128},{65,1},{129,65},{193,129},{66,2},{130,66... | collective-permute-start | bytes 393224 | tf_op jit(solution)/shard_map/ppermute | solution.py:21
  25.8 3.0 %copy-start.2 = (f32[8,8,32,1]{3,2,1,0:T(8,128)S(1)}, f32[8,8,32,1]{3,2,1,0:T(8,128)}, u32[]{:S(2)}) copy-start(f32[8,8,32,1]{3,2,1,0:T(8,128)} %copy.60) | copy-start | bytes 24580
  25.8 3.0 %copy-start.4 = (f32[8,8,32,1]{3,2,1,0:T(8,128)S(1)}, f32[8,8,32,1]{3,2,1,0:T(8,128)}, u32[]{:S(2)}) copy-start(f32[8,8,32,1]{3,2,1,0:T(8,128)} %copy.61) | copy-start | bytes 24580
  88.8 26.3 %collective-permute-start.7 = (f32[8,1,32,128]{3,2,1,0:T(8,128)}, f32[8,1,32,128]{3,2,1,0:T(8,128)S(1)}, u32[]{:S(2)}, u32[]{:S(2)}) collective-permute-start(f32[8,1,32,128]{3,2,1,0:T(8,128)} %get-tuple-element.73), channel_id=1, source_target_pairs={{0,64},{64,128},{128,192},{1,65},{65,129},{129,193},{2,66},{66,130... | collective-permute-start | bytes 393224 | tf_op jit(solution)/shard_map/ppermute | solution.py:20
  92.8 14.7 %collective-permute-start.10 = (f32[8,8,32,1]{2,1,3,0:T(8,128)S(1)}, f32[8,8,32,1]{2,1,3,0:T(8,128)}, u32[]{:S(2)}, u32[]{:S(2)}) collective-permute-start(f32[8,8,32,1]{2,1,3,0:T(8,128)S(1)} %copy.58), channel_id=1, source_target_pairs={{1,0},{2,1},{3,2},{4,3},{5,4},{6,5},{7,6},{9,8},{10,9},{11,10},{12... | collective-permute-start | bytes 24584 | tf_op jit(solution)/shard_map/ppermute | solution.py:21
  96.4 14.9 %collective-permute-start.11 = (f32[8,8,32,1]{2,1,3,0:T(8,128)}, f32[8,8,32,1]{2,1,3,0:T(8,128)}, u32[]{:S(2)}, u32[]{:S(2)}) collective-permute-start(f32[8,8,32,1]{2,1,3,0:T(8,128)} %copy.59), channel_id=1, source_target_pairs={{0,1},{1,2},{2,3},{3,4},{4,5},{5,6},{6,7},{8,9},{9,10},{10,11},{11... | collective-permute-start | bytes 24584 | tf_op jit(solution)/shard_map/ppermute | solution.py:20
  101.5 11.9 %collective-permute-start.8 = (f32[8,8,1,128]{3,2,1,0:T(1,128)}, f32[8,8,1,128]{3,2,1,0:T(1,128)}, u32[]{:S(2)}, u32[]{:S(2)}) collective-permute-start(f32[8,8,1,128]{3,2,1,0:T(1,128)} %get-tuple-element.71), channel_id=1, source_target_pairs={{8,0},{16,8},{24,16},{32,24},{40,32},{48,40},{56,48},{9,1},{17,9},... | collective-permute-start | bytes 98312 | tf_op jit(solution)/shard_map/ppermute | solution.py:21
  103.5 10.8 %collective-permute-start.9 = (f32[8,8,1,128]{3,2,1,0:T(1,128)}, f32[8,8,1,128]{3,2,1,0:T(1,128)}, u32[]{:S(2)}, u32[]{:S(2)}) collective-permute-start(f32[8,8,1,128]{3,2,1,0:T(1,128)} %get-tuple-element.70), channel_id=1, source_target_pairs={{0,8},{8,16},{16,24},{24,32},{32,40},{40,48},{48,56},{1,9},{9,17},... | collective-permute-start | bytes 98312 | tf_op jit(solution)/shard_map/ppermute | solution.py:20
  107.6 8.2 %collective-permute-start.6 = (f32[8,1,32,128]{3,2,1,0:T(8,128)}, f32[8,1,32,128]{3,2,1,0:T(8,128)S(1)}, u32[]{:S(2)}, u32[]{:S(2)}) collective-permute-start(f32[8,1,32,128]{3,2,1,0:T(8,128)} %get-tuple-element.72), channel_id=1, source_target_pairs={{64,0},{128,64},{192,128},{65,1},{129,65},{193,129},{66,2},{130,66... | collective-permute-start | bytes 393224 | tf_op jit(solution)/shard_map/ppermute | solution.py:21
  115.1 1.2 copy-start.1
  115.1 1.5 copy-start.3
where the time goes:
time: 175 us; the launch traced here: 174 us
  blocking collectives  79.4 us (45%)
  local copies, waits for them, and re-layouts  30.8 us (18%)
  starting transfers between devices  28.9 us (17%)
  other arithmetic  16.5 us (9%)
  matrix products  14.1 us (8%)
  waiting for transfers between devices  3.37 us (2%)
    psum x8, blocking collectives, by_axis(): value = lax.psum(value, axis)  79.4 us
    ppermute x6, starting transfers between devices, padded_2(): lax.ppermute(last, axis, up)  19.7 us
    unnamed x30, local copies, waits for them, and re-layouts  18.2 us
    dot_general x16, matrix products, small_dot(): return jnp.dot(left, right, precision=lax.Precision.HIGHEST)  13.3 us
    ppermute x6, starting transfers between devices, padded_2(): lax.ppermute(leading, axis, [(b, a) for a, b in up])  9.2 us
    slice x4, local copies, waits for them, and re-layouts, padded_2(): leading = lax.slice_in_dim(value, 0, width, axis=dim)  6.01 us
    another operation x5, other arithmetic  3.95 us
  transfers between devices with their start and end apart: 12, of which 2 were waited for; matrix products, arithmetic and copies ran while one was open for 12% of the time, Pallas kernels for 0%

commit v1 on v0

--- a/solution.py
+++ b/solution.py
@@ -31,7 +31,7 @@
 
 def by_axis(value, axes):
     for axis in axes:
-        value = lax.psum(value, axis)
+        value = jnp.sum(lax.all_gather(value, axis), axis=0)
     return value
 
 

time: 175 us -> 205 us (1.17)
  blocking collectives: 79.4 us -> 107 us
    all_gather x0 -> x8, blocking collectives: none -> 107 us  [by_axis(): value = jnp.sum(lax.all_gather(value, axis), axis=0)]
    psum x8 -> x0, blocking collectives: 79.4 us -> none  [by_axis(): value = lax.psum(value, axis)]
    unnamed x30 -> x31, local copies, waits for them, and re-layouts: 18.2 us -> 18.7 us
  transfers between devices with their start and end apart: 12 -> 12, of which waited for: 2 -> 1; matrix products, arithmetic and copies ran while one was open for 12% -> 10% of each run, Pallas kernels for 0% -> 0%
where the time goes in v1:
time: 205 us; the launch traced here: 203 us
  blocking collectives  107 us (52%)
  local copies, waits for them, and re-layouts  31.2 us (15%)
  starting transfers between devices  30.3 us (15%)
  other arithmetic  16.6 us (8%)
  matrix products  13.9 us (7%)
  waiting for transfers between devices  2.93 us (1%)
    all_gather x8, blocking collectives, by_axis(): value = jnp.sum(lax.all_gather(value, axis), axis=0)  107 us
    ppermute x6, starting transfers between devices, padded_2(): lax.ppermute(last, axis, up)  21.1 us
    unnamed x31, local copies, waits for them, and re-layouts  18.7 us
    dot_general x16, matrix products, small_dot(): return jnp.dot(left, right, precision=lax.Precision.HIGHEST)  13.2 us
    ppermute x6, starting transfers between devices, padded_2(): lax.ppermute(leading, axis, [(b, a) for a, b in up])  9.2 us
    slice x4, local copies, waits for them, and re-layouts, padded_2(): leading = lax.slice_in_dim(value, 0, width, axis=dim)  6 us
  transfers between devices with their start and end apart: 12, of which 1 were waited for; matrix products, arithmetic and copies ran while one was open for 10% of the time, Pallas kernels for 0%

profile of v1, /device:TPU:8, one launch (start us, length us, event | category | flops | bytes accessed | tf_op | source)
XLA Modules:
  0.0 202.8 jit_solution(9807192866905583547)
XLA Ops:
  0.6 1.7 fusion.71
  2.3 3.4 %collective-permute-start.1 = (f32[8,1,32,128]{3,2,1,0:T(8,128)}, f32[8,1,32,128]{3,2,1,0:T(8,128)S(1)}, u32[]{:S(2)}, u32[]{:S(2)}) collective-permute-start(f32[8,1,32,128]{3,2,1,0:T(8,128)} %get-tuple-element.81), channel_id=1, source_target_pairs={{0,64},{64,128},{128,192},{1,65},{65,129},{129,193},{2,66},{66,130... | collective-permute-start | bytes 393224 | tf_op jit(solution)/shard_map/ppermute | solution.py:20
  5.7 1.9 fusion.69
  7.7 1.0 copy.80
  8.7 1.3 collective-permute-start.4
  10.0 1.0 copy.81
  11.0 4.7 %collective-permute-start.5 = (f32[8,8,32,1]{2,1,3,0:T(8,128)}, f32[8,8,32,1]{2,1,3,0:T(8,128)S(1)}, u32[]{:S(2)}, u32[]{:S(2)}) collective-permute-start(f32[8,8,32,1]{2,1,3,0:T(8,128)} %copy.81), channel_id=1, source_target_pairs={{0,1},{1,2},{2,3},{3,4},{4,5},{5,6},{6,7},{8,9},{9,10},{10,11},{11... | collective-permute-start | bytes 24584 | tf_op jit(solution)/shard_map/ppermute | solution.py:20
  15.8 1.9 collective-permute-start.2
  17.7 2.4 %collective-permute-start.3 = (f32[8,8,1,128]{3,2,1,0:T(1,128)S(1)}, f32[8,8,1,128]{3,2,1,0:T(1,128)S(1)}, u32[]{:S(2)}, u32[]{:S(2)}) collective-permute-start(f32[8,8,1,128]{3,2,1,0:T(1,128)S(1)} %get-tuple-element.78), channel_id=1, source_target_pairs={{0,8},{8,16},{16,24},{24,32},{32,40},{40,48},{48,56},{1,9},{9,17},... | collective-permute-start | bytes 98312 | tf_op jit(solution)/shard_map/ppermute | solution.py:20
  20.8 1.3 collective-permute-start
  22.1 2.2 %copy.85 = f32[8,8,32,1]{3,2,1,0:T(8,128)} copy(f32[8,8,32,1]{2,1,3,0:T(8,128)} %collective-permute-done.4) | data formatting | bytes 16384
  24.3 1.4 copy.86
  25.9 2.9 %collective-permute-done = f32[8,1,32,128]{3,2,1,0:T(8,128)S(1)} collective-permute-done((f32[8,1,32,128]{3,2,1,0:T(8,128)S(1)}, f32[8,1,32,128]{3,2,1,0:T(8,128)S(1)}, u32[]{:S(2)}, u32[]{:S(2)}) %collective-permute-start) | collective-permute-done | bytes 131104 | tf_op jit(solution)/shard_map/ppermute | solution.py:21
  28.9 1.2 fusion.29
  30.7 2.8 %fusion.6 = f32[16,16]{1,0:T(8,128)S(1)} fusion(f32[8,32768]{1,0:T(8,128)S(1)} %bitcast.103, f32[8,32768]{1,0:T(8,128)S(1)} %bitcast.101), kind=kOutput, calls=%fused_computation.7 | convolution fusion | flops 101187584 | bytes 2098176 | tf_op jit(solution)/shard_map/dot_general | solution.py:52
  33.4 12.0 %all-gather = f32[64,16]{1,0:T(8,128)S(1)} all-gather(f32[16,16]{1,0:T(8,128)S(1)} %fusion.6), channel_id=2, replica_groups=mesh['gx'=4,'gy_0'=4,'gy_1'=2,'gz'=8] {'gx'}, dimensions={0}, use_global_device_ids=true | all-gather | bytes 5120 | tf_op jit(solution)/shard_map/all_gather | solution.py:34
  45.4 12.1 %all-gather.1 = f32[64,16]{1,0:T(8,128)S(1)} all-gather(f32[16,16]{1,0:T(8,128)S(1)} %reduce_sum.81), channel_id=3, replica_groups=mesh['gx'=4,'gy_0'=4,'gy_1'=2,'gz'=8] {'gy_0'}, dimensions={0}, use_global_device_ids=true | all-gather | bytes 5120 | tf_op jit(solution)/shard_map/all_gather | solution.py:34
  57.5 1.8 all-gather.2
  59.3 29.2 %all-gather.3 = f32[128,16]{1,0:T(8,128)S(1)} all-gather(f32[16,16]{1,0:T(8,128)S(1)} %reduce_sum.83), channel_id=5, replica_groups=mesh['gx'=4,'gy_0'=4,'gy_1'=2,'gz'=8] {'gz'}, dimensions={0}, use_global_device_ids=true | all-gather | bytes 9216 | tf_op jit(solution)/shard_map/all_gather | solution.py:34
  88.6 0.7 cholesky.94
  89.4 0.6 compare_reduce_fusion.2
  90.0 0.6 fusion.58
  90.7 0.6 custom-call.17
  91.7 1.5 fusion.65
  93.2 1.5 fusion.64
  95.4 0.7 cholesky.105
  96.1 0.6 compare_reduce_fusion.1
  96.8 0.6 select_bitcast_fusion.1
  98.2 1.0 convolution_subtract_fusion
  99.2 1.0 fusion.75
  100.4 1.7 fusion.66
  102.1 0.7 fusion.68
  102.8 3.1 %collective-permute-start.7 = (f32[8,1,32,128]{3,2,1,0:T(8,128)}, f32[8,1,32,128]{3,2,1,0:T(8,128)S(1)}, u32[]{:S(2)}, u32[]{:S(2)}) collective-permute-start(f32[8,1,32,128]{3,2,1,0:T(8,128)} %get-tuple-element.75), channel_id=1, source_target_pairs={{0,64},{64,128},{128,192},{1,65},{65,129},{129,193},{2,66},{66,130... | collective-permute-start | bytes 393224 | tf_op jit(solution)/shard_map/ppermute | solution.py:20
  105.9 0.7 fusion.67
  106.6 1.7 copy.83
  108.3 1.3 collective-permute-start.10
  109.6 2.3 %copy.84 = f32[8,8,32,1]{2,1,3,0:T(8,128)} copy(f32[8,8,32,1]{3,0,2,1:T(8,128)} %get-tuple-element.71) | data formatting | bytes 16384
  111.8 5.1 %collective-permute-start.11 = (f32[8,8,32,1]{2,1,3,0:T(8,128)}, f32[8,8,32,1]{2,1,3,0:T(8,128)}, u32[]{:S(2)}, u32[]{:S(2)}) collective-permute-start(f32[8,8,32,1]{2,1,3,0:T(8,128)} %copy.84), channel_id=1, source_target_pairs={{0,1},{1,2},{2,3},{3,4},{4,5},{5,6},{6,7},{8,9},{9,10},{10,11},{11... | collective-permute-start | bytes 24584 | tf_op jit(solution)/shard_map/ppermute | solution.py:20
  117.0 1.9 collective-permute-start.8
  118.9 2.4 %collective-permute-start.9 = (f32[8,8,1,128]{3,2,1,0:T(1,128)}, f32[8,8,1,128]{3,2,1,0:T(1,128)}, u32[]{:S(2)}, u32[]{:S(2)}) collective-permute-start(f32[8,8,1,128]{3,2,1,0:T(1,128)} %get-tuple-element.72), channel_id=1, source_target_pairs={{0,8},{8,16},{16,24},{24,32},{32,40},{40,48},{48,56},{1,9},{9,17},... | collective-permute-start | bytes 98312 | tf_op jit(solution)/shard_map/ppermute | solution.py:20
  121.9 0.7 and_reduce_fusion
  123.0 1.5 collective-permute-start.6
  124.5 2.2 %copy.87 = f32[8,8,32,1]{3,2,1,0:T(8,128)} copy(f32[8,8,32,1]{2,1,3,0:T(8,128)} %collective-permute-done.10) | data formatting | bytes 16384
  126.7 2.2 %copy.88 = f32[8,8,32,1]{3,2,1,0:T(8,128)} copy(f32[8,8,32,1]{2,1,3,0:T(8,128)} %collective-permute-done.11) | data formatting | bytes 16384
  128.9 0.8 pad.51
  129.7 0.8 pad.52
  130.8 1.0 copy-done.1
  132.1 1.2 fusion.21
  133.8 3.0 %fusion.14 = f32[1,24,8]{1,2,0:T(8,128)S(1)} fusion(f32[8,32768]{1,0:T(8,128)S(1)} %bitcast.105, f32[8,32768]{1,0:T(8,128)S(1)} %fusion.75, f32[8,32768]{1,0:T(8,128)S(1)} %fusion.64), kind=kOutput, calls=%fused_computation.15 | convolution fusion | flops 77070336 | bytes 3146496 | tf_op jit(solution)/shard_map/dot_general | solution.py:52
  136.9 12.6 %all-gather.8 = f32[4,24,8]{1,2,0:T(8,128)S(1)} all-gather(f32[1,24,8]{1,2,0:T(8,128)S(1)} %fusion.14), channel_id=6, replica_groups=mesh['gx'=4,'gy_0'=4,'gy_1'=2,'gz'=8] {'gx'}, dimensions={0}, use_global_device_ids=true | all-gather | bytes 3840 | tf_op jit(solution)/shard_map/all_gather | solution.py:34
  149.5 12.6 %all-gather.9 = f32[4,24,8]{1,2,0:T(8,128)S(1)} all-gather(f32[1,24,8]{1,2,0:T(8,128)S(1)} %bitcast.111), channel_id=7, replica_groups=mesh['gx'=4,'gy_0'=4,'gy_1'=2,'gz'=8] {'gy_0'}, dimensions={0}, use_global_device_ids=true | all-gather | bytes 3840 | tf_op jit(solution)/shard_map/all_gather | solution.py:34
  162.1 1.8 all-gather.10
  163.9 24.7 %all-gather.11 = f32[8,24,8]{1,2,0:T(8,128)S(1)} all-gather(f32[1,24,8]{1,2,0:T(8,128)S(1)} %bitcast.110), channel_id=9, replica_groups=mesh['gx'=4,'gy_0'=4,'gy_1'=2,'gz'=8] {'gz'}, dimensions={0}, use_global_device_ids=true | all-gather | bytes 6912 | tf_op jit(solution)/shard_map/all_gather | solution.py:34
  188.8 0.7 cholesky.116
  189.6 0.6 compare_reduce_fusion
  190.2 0.6 select_bitcast_fusion
  190.9 2.0 dynamic-slice_select_fusion
  192.9 1.7 scatter.20
  195.3 1.5 cholesky.41
  196.8 0.6 compare_reduce_fusion.3
  197.4 0.6 fusion.35
  198.1 1.2 custom-call.15
  200.0 1.1 fusion.10
  201.6 1.2 copy.76
  (79 shorter events, 8.2 us)
Async XLA Ops:
  2.3 23.5 %collective-permute-start.1 = (f32[8,1,32,128]{3,2,1,0:T(8,128)}, f32[8,1,32,128]{3,2,1,0:T(8,128)S(1)}, u32[]{:S(2)}, u32[]{:S(2)}) collective-permute-start(f32[8,1,32,128]{3,2,1,0:T(8,128)} %get-tuple-element.81), channel_id=1, source_target_pairs={{0,64},{64,128},{128,192},{1,65},{65,129},{129,193},{2,66},{66,130... | collective-permute-start | bytes 393224 | tf_op jit(solution)/shard_map/ppermute | solution.py:20
  7.6 8.1 %copy-start = (f32[8,8,32,128]{3,2,1,0:T(8,128)S(1)}, f32[8,8,32,128]{3,2,1,0:T(8,128)}, u32[]{:S(2)}) copy-start(f32[8,8,32,128]{3,2,1,0:T(8,128)} %param.15) | copy-start | bytes 3145732
  7.6 12.5 %copy-start.5 = (f32[8,32,128]{2,1,0:T(8,128)S(1)}, f32[8,32,128]{2,1,0:T(8,128)}, u32[]{:S(2)}) copy-start(f32[8,32,128]{2,1,0:T(8,128)} %param.16) | copy-start | bytes 393220
  8.7 12.1 %collective-permute-start.4 = (f32[8,8,32,1]{2,1,3,0:T(8,128)}, f32[8,8,32,1]{2,1,3,0:T(8,128)}, u32[]{:S(2)}, u32[]{:S(2)}) collective-permute-start(f32[8,8,32,1]{2,1,3,0:T(8,128)} %copy.80), channel_id=1, source_target_pairs={{1,0},{2,1},{3,2},{4,3},{5,4},{6,5},{7,6},{9,8},{10,9},{11,10},{12... | collective-permute-start | bytes 24584 | tf_op jit(solution)/shard_map/ppermute | solution.py:21
  11.0 9.8 %copy-start.6 = (f32[8,1,32,128]{3,2,1,0:T(8,128)S(1)}, f32[8,1,32,128]{3,2,1,0:T(8,128)}, u32[]{:S(2)}) copy-start(f32[8,1,32,128]{3,2,1,0:T(8,128)} %get-tuple-element.80) | copy-start | bytes 393220
  11.0 13.3 %collective-permute-start.5 = (f32[8,8,32,1]{2,1,3,0:T(8,128)}, f32[8,8,32,1]{2,1,3,0:T(8,128)S(1)}, u32[]{:S(2)}, u32[]{:S(2)}) collective-permute-start(f32[8,8,32,1]{2,1,3,0:T(8,128)} %copy.81), channel_id=1, source_target_pairs={{0,1},{1,2},{2,3},{3,4},{4,5},{5,6},{6,7},{8,9},{9,10},{10,11},{11... | collective-permute-start | bytes 24584 | tf_op jit(solution)/shard_map/ppermute | solution.py:20
  15.8 10.0 %collective-permute-start.2 = (f32[8,8,1,128]{3,2,1,0:T(1,128)S(1)}, f32[8,8,1,128]{3,2,1,0:T(1,128)S(1)}, u32[]{:S(2)}, u32[]{:S(2)}) collective-permute-start(f32[8,8,1,128]{3,2,1,0:T(1,128)S(1)} %get-tuple-element.79), channel_id=1, source_target_pairs={{8,0},{16,8},{24,16},{32,24},{40,32},{48,40},{56,48},{9,1},{17,9},... | collective-permute-start | bytes 98312 | tf_op jit(solution)/shard_map/ppermute | solution.py:21
  17.7 8.1 %collective-permute-start.3 = (f32[8,8,1,128]{3,2,1,0:T(1,128)S(1)}, f32[8,8,1,128]{3,2,1,0:T(1,128)S(1)}, u32[]{:S(2)}, u32[]{:S(2)}) collective-permute-start(f32[8,8,1,128]{3,2,1,0:T(1,128)S(1)} %get-tuple-element.78), channel_id=1, source_target_pairs={{0,8},{8,16},{16,24},{24,32},{32,40},{40,48},{48,56},{1,9},{9,17},... | collective-permute-start | bytes 98312 | tf_op jit(solution)/shard_map/ppermute | solution.py:20
  20.8 8.0 %collective-permute-start = (f32[8,1,32,128]{3,2,1,0:T(8,128)S(1)}, f32[8,1,32,128]{3,2,1,0:T(8,128)S(1)}, u32[]{:S(2)}, u32[]{:S(2)}) collective-permute-start(f32[8,1,32,128]{3,2,1,0:T(8,128)S(1)} %copy-done.6), channel_id=1, source_target_pairs={{64,0},{128,64},{192,128},{65,1},{129,65},{193,129},{66,2},{130,66... | collective-permute-start | bytes 393224 | tf_op jit(solution)/shard_map/ppermute | solution.py:21
  25.8 3.0 %copy-start.2 = (f32[8,8,32,1]{3,2,1,0:T(8,128)S(1)}, f32[8,8,32,1]{3,2,1,0:T(8,128)}, u32[]{:S(2)}) copy-start(f32[8,8,32,1]{3,2,1,0:T(8,128)} %copy.85) | copy-start | bytes 24580
  25.8 3.0 %copy-start.4 = (f32[8,8,32,1]{3,2,1,0:T(8,128)S(1)}, f32[8,8,32,1]{3,2,1,0:T(8,128)}, u32[]{:S(2)}) copy-start(f32[8,8,32,1]{3,2,1,0:T(8,128)} %copy.86) | copy-start | bytes 24580
  102.8 27.7 %collective-permute-start.7 = (f32[8,1,32,128]{3,2,1,0:T(8,128)}, f32[8,1,32,128]{3,2,1,0:T(8,128)S(1)}, u32[]{:S(2)}, u32[]{:S(2)}) collective-permute-start(f32[8,1,32,128]{3,2,1,0:T(8,128)} %get-tuple-element.75), channel_id=1, source_target_pairs={{0,64},{64,128},{128,192},{1,65},{65,129},{129,193},{2,66},{66,130... | collective-permute-start | bytes 393224 | tf_op jit(solution)/shard_map/ppermute | solution.py:20
  108.3 14.7 %collective-permute-start.10 = (f32[8,8,32,1]{2,1,3,0:T(8,128)S(1)}, f32[8,8,32,1]{2,1,3,0:T(8,128)}, u32[]{:S(2)}, u32[]{:S(2)}) collective-permute-start(f32[8,8,32,1]{2,1,3,0:T(8,128)S(1)} %copy.83), channel_id=1, source_target_pairs={{1,0},{2,1},{3,2},{4,3},{5,4},{6,5},{7,6},{9,8},{10,9},{11,10},{12... | collective-permute-start | bytes 24584 | tf_op jit(solution)/shard_map/ppermute | solution.py:21
  111.8 14.9 %collective-permute-start.11 = (f32[8,8,32,1]{2,1,3,0:T(8,128)}, f32[8,8,32,1]{2,1,3,0:T(8,128)}, u32[]{:S(2)}, u32[]{:S(2)}) collective-permute-start(f32[8,8,32,1]{2,1,3,0:T(8,128)} %copy.84), channel_id=1, source_target_pairs={{0,1},{1,2},{2,3},{3,4},{4,5},{5,6},{6,7},{8,9},{9,10},{10,11},{11... | collective-permute-start | bytes 24584 | tf_op jit(solution)/shard_map/ppermute | solution.py:20
  117.0 11.9 %collective-permute-start.8 = (f32[8,8,1,128]{3,2,1,0:T(1,128)}, f32[8,8,1,128]{3,2,1,0:T(1,128)}, u32[]{:S(2)}, u32[]{:S(2)}) collective-permute-start(f32[8,8,1,128]{3,2,1,0:T(1,128)} %get-tuple-element.73), channel_id=1, source_target_pairs={{8,0},{16,8},{24,16},{32,24},{40,32},{48,40},{56,48},{9,1},{17,9},... | collective-permute-start | bytes 98312 | tf_op jit(solution)/shard_map/ppermute | solution.py:21
  118.9 10.8 %collective-permute-start.9 = (f32[8,8,1,128]{3,2,1,0:T(1,128)}, f32[8,8,1,128]{3,2,1,0:T(1,128)}, u32[]{:S(2)}, u32[]{:S(2)}) collective-permute-start(f32[8,8,1,128]{3,2,1,0:T(1,128)} %get-tuple-element.72), channel_id=1, source_target_pairs={{0,8},{8,16},{16,24},{24,32},{32,40},{40,48},{48,56},{1,9},{9,17},... | collective-permute-start | bytes 98312 | tf_op jit(solution)/shard_map/ppermute | solution.py:20
  123.0 7.7 %collective-permute-start.6 = (f32[8,1,32,128]{3,2,1,0:T(8,128)}, f32[8,1,32,128]{3,2,1,0:T(8,128)S(1)}, u32[]{:S(2)}, u32[]{:S(2)}) collective-permute-start(f32[8,1,32,128]{3,2,1,0:T(8,128)} %get-tuple-element.74), channel_id=1, source_target_pairs={{64,0},{128,64},{192,128},{65,1},{129,65},{193,129},{66,2},{130,66... | collective-permute-start | bytes 393224 | tf_op jit(solution)/shard_map/ppermute | solution.py:21
  130.5 1.2 copy-start.1
  130.5 1.5 copy-start.3
